TPU v7x, 32 devices: a whole 2x2x4 slice. The times are simulated.
32 devices in a mesh: section: 2 (over y), ep: 16 (over z, x, core).
Axes of the slice: x: 2, y: 2, z: 4, core: 2. Of those that a mesh axis runs over, the one named last changes fastest.
Arguments:
- inputs: bfloat16 [2, 2048, 1536], P('section', 'ep'), may hold values from -6 to 6
- upstream: bfloat16 [2, 2048, 1536], P('section', 'ep'), may hold values from -6 to 6
- gate_saved: bfloat16 [2, 2048, 8, 384], P('section', 'ep'), may hold values from -6 to 6
- expert_ids: int32 [2, 2048, 8], P('section', 'ep'), may hold values from 0 to 31, all different within a row; in each aligned block of 128 rows (0 to 127, 128 to 255, ..., all dimensions but the last counted through in order) at most 48 rows name the same one
- route_weights: float32 [2, 2048, 8], P('section', 'ep'), may hold values from 0.05 to 0.5
- w_up: bfloat16 [2, 32, 1536, 384], P('section', 'ep'), may hold values from -0.15625 to 0.15625
- w_down: bfloat16 [2, 32, 384, 1536], P('section', 'ep'), may hold values from -0.3125 to 0.3125
Outputs:
- delivered: bfloat16 [2, 2048, 1536], P('section', 'ep')
- grad_up: bfloat16 [2, 32, 1536, 384], P('section', 'ep')
- grad_down: bfloat16 [2, 32, 384, 1536], P('section', 'ep')
Inputs may be any that keep to these rules, and one draw needn't show every extreme that they name: `expert_ids`: each row names 8 different experts. In the rows of one device no expert is named more than 48 times, and in every draw some expert is named exactly 48 times in the rows of some device; every expert is named somewhere.
All inputs are finite; a program needn't handle non-finite values.
Results may differ from a plain program's by a relative error of at most 0.012.
Values may be sent and summed in bfloat16 or wider, within the bound.
A program may use at most 192 MiB of HBM per device.

v0:
```python
import jax
import jax.numpy as jnp
from jax import lax
from jax.sharding import PartitionSpec as P

BF16 = jnp.bfloat16
F32 = jnp.float32


def from_behind(block, axis, distance):
    devices = range(lax.axis_size(axis))
    route = [((i - distance) % len(devices), i) for i in devices]
    return lax.ppermute(block, axis, route)


def body(inputs, upstream, gate_saved, expert_ids, route_weights, w_up, w_down):
    ep = lax.axis_size("ep")
    local = w_up.shape[1]
    experts = local * ep
    toks, top = expert_ids.shape[1:]
    cap = 3 * toks * top // (2 * experts)
    width = inputs.shape[2]
    ff = w_up.shape[3]
    routing = jnp.concatenate([expert_ids[0].astype(F32), route_weights[0]], axis=1)
    routing_all = lax.all_gather(routing, "ep", axis=0, tiled=False)
    ids = expert_ids[0]
    hit = ids[:, :, None] == jnp.arange(experts, dtype=jnp.int32)
    member = jnp.any(hit, axis=1).astype(BF16)
    lower = (jnp.arange(toks)[:, None] > jnp.arange(toks)[None, :]).astype(BF16)
    rank = jnp.dot(lower, member, preferred_element_type=F32)
    place = jnp.sum(jnp.where(hit, rank[:, None, :], 0.0), axis=2)
    slot = (ids * cap + place.astype(jnp.int32)).reshape(1, toks * top)
    pick = (jnp.arange(experts * cap, dtype=jnp.int32)[:, None] == slot).astype(BF16)
    gate_send = jnp.dot(pick, gate_saved[0].reshape(toks * top, ff), preferred_element_type=F32)
    gate_send = gate_send.astype(BF16).reshape(ep, local, cap, ff)
    gate_recv = lax.all_to_all(gate_send, "ep", split_axis=0, concat_axis=0, tiled=True)
    cot = from_behind(upstream, "section", -1)[0]
    x_all = lax.all_gather(inputs[0], "ep", axis=0, tiled=True)
    c_all = lax.all_gather(cot, "ep", axis=0, tiled=True)
    me = lax.axis_index("ep")
    mine = (me * local + jnp.arange(local)).astype(F32)
    hits = routing_all[:, :, :top, None] == mine
    weight = jnp.sum(jnp.where(hits, routing_all[:, :, top:, None], 0.0), axis=2)
    members = jnp.any(hits, axis=2)
    ranks = jnp.einsum("ab,sbe->sae", lower, members.astype(BF16), preferred_element_type=F32)
    ranks = jnp.where(members, ranks, -1.0)
    spread = (ranks[:, :, :, None] == jnp.arange(cap).astype(F32)).astype(BF16)
    gate = jnp.einsum("stec,secf->stef", spread, gate_recv, preferred_element_type=F32)
    act = jax.nn.silu(gate).reshape(ep * toks, local, ff)
    weight = weight.reshape(ep * toks, local, 1)
    act_w = act * weight
    up = w_up[0]
    down = w_down[0]
    up_cat = jnp.transpose(up, (1, 0, 2)).reshape(width, local * ff)
    down_cat = down.reshape(local * ff, width)
    act_w = act_w.reshape(ep * toks, local * ff)
    u = jnp.dot(x_all, up_cat, preferred_element_type=F32)
    hidden = (act_w * u).astype(BF16)
    h = lax.dot_general(c_all, down_cat, (((1,), (1,)), ((), ())), preferred_element_type=F32)
    g = (act_w * h).astype(BF16)
    part = lax.dot_general(g, up_cat, (((1,), (1,)), ((), ())), preferred_element_type=F32)
    grad = lax.psum_scatter(part.astype(BF16), "ep", scatter_dimension=0, tiled=True)
    delivered = from_behind(grad[None], "section", -1)
    grad_down = lax.dot_general(hidden, c_all, (((0,), (0,)), ((), ())), preferred_element_type=F32)
    grad_up = jnp.stack(
        [
            lax.dot_general(
                x_all,
                g[:, e * ff : (e + 1) * ff],
                (((0,), (0,)), ((), ())),
                preferred_element_type=F32,
            )
            for e in range(local)
        ]
    )
    return (
        delivered,
        grad_up.astype(BF16)[None],
        grad_down.astype(BF16).reshape(1, local, ff, width),
    )


def solution(mesh):
    return jax.shard_map(
        body,
        mesh=mesh,
        in_specs=(
            P("section", "ep", None),
            P("section", "ep", None),
            P("section", "ep", None, None),
            P("section", "ep", None),
            P("section", "ep", None),
            P("section", "ep", None, None),
            P("section", "ep", None, None),
        ),
        out_specs=(
            P("section", "ep", None),
            P("section", "ep", None, None),
            P("section", "ep", None, None),
        ),
        check_vma=False,
    )
```

profile of v0, /device:TPU:0, one launch (start us, length us, event | category | flops | bytes accessed | tf_op | source)
XLA Modules:
  0.0 272.7 jit_solution(5686237098454286970)
XLA Ops:
  7.2 0.0 copy-start
  7.2 0.0 all-gather.6.cloned.1.call-start
  7.2 3.1 %collective-permute-start = (bf16[1,128,1536]{2,1,0:T(8,128)(2,1)}, bf16[1,128,1536]{2,1,0:T(8,128)(2,1)S(1)}, u32[]{:S(2)}, u32[]{:S(2)}) collective-permute-start(bf16[1,128,1536]{2,1,0:T(8,128)(2,1)} %param.8), channel_id=1, source_target_pairs={{16,0},{0,16},{17,1},{1,17},{18,2},{2,18},{19,3},{3,19},{20,4},{4,... | collective-permute-start | bytes 1179656 | tf_op jit(solution)/shard_map/ppermute | solution.py:13
  10.3 9.3 %collective-permute-done = bf16[1,128,1536]{2,1,0:T(8,128)(2,1)S(1)} collective-permute-done((bf16[1,128,1536]{2,1,0:T(8,128)(2,1)}, bf16[1,128,1536]{2,1,0:T(8,128)(2,1)S(1)}, u32[]{:S(2)}, u32[]{:S(2)}) %collective-permute-start) | collective-permute-done | bytes 393248 | tf_op jit(solution)/shard_map/ppermute | solution.py:13
  19.6 0.0 copy-start.4
  19.6 0.7 copy-done.4
  20.4 0.0 all-gather.6.cloned.1.call-update
  20.4 0.0 all-gather.8.cloned.1.call-start
  20.4 0.7 all-gather.8.cloned.1.call-update
  21.1 0.7 bitcast_convert_fusion
  21.8 0.1 copy.35
  21.9 0.1 mul.41
  22.0 0.7 fusion.45
  22.7 0.1 fusion.47
  22.9 0.7 select_reduce_fusion
  23.6 0.1 copy.36
  23.7 0.1 convert_element_type.56
  23.8 0.0 copy-start.5
  23.8 4.0 %fusion.22 = bf16[1536,384]{1,0:T(8,128)(2,1)} fusion(s32[1024]{0:T(1024)S(1)} %add.23, bf16[1,128,8,384]{3,2,1,0:T(8,128)(2,1)} %param.9), kind=kOutput, calls=%fused_computation.22 | convolution fusion | flops 1210122240 | bytes 1970176 | tf_op jit(solution)/shard_map/dot_general | solution.py:34
  27.8 6.2 %all-to-all-start = ((bf16[16,2,48,384]{3,2,1,0:T(8,128)(2,1)}), bf16[16,2,48,384]{3,2,1,0:T(8,128)(2,1)}, u32[]{:S(2)}, u32[]{:S(2)}) async-start(bf16[16,2,48,384]{3,2,1,0:T(8,128)(2,1)} %bitcast.2), calls=%async_computation | async-start | bytes 2359296 | tf_op jit(solution)/shard_map/all_to_all | solution.py:36
  34.0 0.0 reduce-scatter.2.cloned.1.call-start
  34.0 0.0 copy-done.5
  34.0 45.0 %all-gather = f32[2048,16]{0,1:T(8,128)S(1)} all-gather(f32[128,16]{0,1:T(8,128)S(1)} %pad_maximum_fusion.1), channel_id=2, replica_groups=mesh['section'=2,'ep'=16] {'ep'}, dimensions={0}, use_global_device_ids=true | all-gather | bytes 139264 | tf_op jit(solution)/shard_map/all_gather | solution.py:25
  79.1 0.1 compare_reduce_fusion
  79.2 0.1 fusion.37
  79.4 0.1 fusion.44
  79.6 0.4 copy.43
  79.9 4.8 %mul.45 = f32[2048,2,384]{2,1,0:T(2,128)S(1)} broadcast(f32[2048,2]{1,0:T(8,128)S(1)} %copy.43), dimensions={0,1} | broadcast | bytes 6307840 | tf_op jit(solution)/shard_map/mul | solution.py:51
  84.8 3.0 %copy.53 = f32[256,8,2,384]{3,1,2,0:T(8,128)} copy(f32[256,8,2,384]{3,2,1,0:T(2,128)S(1)} %bitcast.86) | data formatting | bytes 12582912
  87.8 4.3 %copy.45 = bf16[1,2,1536,384]{2,3,1,0:T(8,128)(2,1)} copy(bf16[1,2,1536,384]{3,2,1,0:T(8,128)(2,1)} %param.12) | data formatting | bytes 4718592 | tf_op args[5]
  92.1 0.0 all-to-all-done
  92.1 5.8 %bitcast_multiply_fusion = f32[16,128,2,384]{1,3,2,0:T(8,128)} fusion(bf16[16,2,48,384]{3,2,1,0:T(8,128)(2,1)} %all-to-all-done, f32[16,128,2]{1,2,0:T(2,128)S(1)} %copy.40, f32[48]{0:T(128)S(1)} %iota_convert_fusion), kind=kOutput, calls=%fused_computation.11 | convolution fusion | flops 157483008 | bytes 7487680 | tf_op jit(solution)/shard_map/stec,secf->stef/dot_general | solution.py:48
  97.8 10.3 %copy.47 = f32[16,128,2,384]{3,2,1,0:T(2,128)} copy(f32[16,128,2,384]{1,3,2,0:T(8,128)} %bitcast_multiply_fusion) | data formatting | bytes 12582912 | tf_op jit(solution)/shard_map/reshape | solution.py:49
  108.2 6.1 %copy.52 = f32[256,8,2,384]{3,1,2,0:T(8,128)} copy(f32[256,8,2,384]{3,2,1,0:T(2,128)} %bitcast.87) | data formatting | bytes 12582912
  114.2 0.0 all-gather.6.cloned.1.call-done
  114.2 0.0 copy-done
  114.2 0.0 copy-start.2
  114.2 10.2 %multiply_convert_fusion.1 = bf16[2048,768]{1,0:T(8,128)(2,1)S(1)} fusion(bf16[768,1536]{1,0:T(8,128)(2,1)S(1)} %bitcast.85, bf16[1,2048,1536]{2,1,0:T(8,128)(2,1)} %all-gather.6.cloned.1.call-done, f32[2048,768]{1,0:T(8,128)} %bitcast.90, f32[2048,768]{1,0:T(8,128)} %bitcast.88), kind=kOutput, calls=%fused_computation.17 | convolution fusion | flops 4836556800 | bytes 24379392 | tf_op jit(solution)/shard_map/dot_general | solution.py:59
  124.5 0.0 copy-start.6
  124.5 1.6 copy-done.6
  126.1 0.0 copy-done.2
  126.1 6.9 %convolution_convert_fusion = bf16[2048,1536]{1,0:T(8,128)(2,1)} fusion(bf16[2048,768]{1,0:T(8,128)(2,1)S(1)} %multiply_convert_fusion.1, bf16[1536,768]{0,1:T(8,128)(2,1)S(1)} %bitcast.92), kind=kOutput, calls=%fused_computation | convolution fusion | flops 4834983936 | bytes 11796480 | tf_op jit(solution)/shard_map/dot_general | solution.py:61
  133.0 0.0 reduce-scatter.2.cloned.1.call-update
  133.1 0.0 copy-start.3
  133.1 30.3 %all-gather.8.cloned.1.call-done = bf16[1,2048,1536]{2,1,0:T(8,128)(2,1)} async-done(((bf16[1,128,1536]{2,1,0:T(8,128)(2,1)}), bf16[1,2048,1536]{2,1,0:T(8,128)(2,1)}) %all-gather.8.cloned.1.call-update) | async-done | bytes 6291472 | tf_op jit(solution)/shard_map/all_gather | solution.py:38
  163.4 5.9 %fusion.29 = bf16[1,1,1536,384]{2,3,1,0:T(8,128)(2,1)S(1)} fusion(bf16[1,2048,1536]{2,1,0:T(8,128)(2,1)} %all-gather.8.cloned.1.call-done, bf16[2048,768]{1,0:T(8,128)(2,1)} %copy-done.6), kind=kOutput, calls=%fused_computation.25 | convolution fusion | flops 2416508928 | bytes 9043968 | tf_op jit(solution)/shard_map/dot_general | solution.py:67
  169.3 0.0 copy-done.3
  169.3 30.7 %fusion.18 = bf16[768,1536]{1,0:T(8,128)(2,1)} fusion(bf16[1,2048,1536]{2,1,0:T(8,128)(2,1)} %all-gather.6.cloned.1.call-done, bf16[1536,768]{0,1:T(8,128)(2,1)S(1)} %bitcast.93, bf16[1,2048,1536]{2,1,0:T(8,128)(2,1)} %all-gather.8.cloned.1.call-done, f32[2048,768]{1,0:T(8,128)} %bitcast.91, f32[2048,768]{1,0:T(8,128)} %bitcast.89), kind=kOutput, calls=%fused_computation.20 | convolution fusion | flops 9669574656 | bytes 29884416 | tf_op jit(solution)/shard_map/dot_general | solution.py:64
  200.0 51.1 %reduce-scatter.2.cloned.1.call-done = bf16[128,1536]{1,0:T(8,128)(2,1)} async-done(((bf16[2048,1536]{1,0:T(8,128)(2,1)}), bf16[128,1536]{1,0:T(8,128)(2,1)}) %reduce-scatter.2.cloned.1.call-update) | async-done | bytes 393232 | tf_op jit(solution)/shard_map/reduce_scatter | solution.py:62
  251.1 1.5 collective-permute-start.1
  252.6 5.9 %fusion.32 = bf16[1,1,1536,384]{2,3,1,0:T(8,128)(2,1)S(1)} fusion(bf16[1,2048,1536]{2,1,0:T(8,128)(2,1)} %all-gather.8.cloned.1.call-done, bf16[2048,768]{1,0:T(8,128)(2,1)} %copy-done.6), kind=kOutput, calls=%fused_computation.26 | convolution fusion | flops 2416508928 | bytes 9043968 | tf_op jit(solution)/shard_map/dot_general | solution.py:67
  258.5 0.0 copy-start.1
  258.5 1.6 pad_maximum_fusion
  260.2 4.3 %copy.46 = bf16[1,2,1536,384]{3,2,1,0:T(8,128)(2,1)} copy(bf16[1,2,1536,384]{2,3,1,0:T(8,128)(2,1)} %pad_maximum_fusion) | data formatting | bytes 4718592
  264.4 0.0 collective-permute-done.1
  264.4 1.8 copy.57
  266.2 0.0 copy-done.1
  (10 shorter events, 0.1 us)
Async XLA Ops:
  7.2 107.1 %copy-start = (bf16[1,2,384,1536]{3,2,1,0:T(8,128)(2,1)S(1)}, bf16[1,2,384,1536]{3,2,1,0:T(8,128)(2,1)}, u32[]{:S(2)}) copy-start(bf16[1,2,384,1536]{3,2,1,0:T(8,128)(2,1)} %param.13) | copy-start | bytes 7077892
  7.2 107.1 %all-gather.6.cloned.1.call-start = ((), (), s32[]{:S(2)}) async-start(), calls=%async_computation.3 | async-start | bytes 6684672 | tf_op jit(solution)/shard_map/all_gather | solution.py:39
  7.2 12.4 %collective-permute-start = (bf16[1,128,1536]{2,1,0:T(8,128)(2,1)}, bf16[1,128,1536]{2,1,0:T(8,128)(2,1)S(1)}, u32[]{:S(2)}, u32[]{:S(2)}) collective-permute-start(bf16[1,128,1536]{2,1,0:T(8,128)(2,1)} %param.8), channel_id=1, source_target_pairs={{16,0},{0,16},{17,1},{1,17},{18,2},{2,18},{19,3},{3,19},{20,4},{4,... | collective-permute-start | bytes 1179656 | tf_op jit(solution)/shard_map/ppermute | solution.py:13
  19.6 0.7 copy-start.4
  20.4 143.0 %all-gather.8.cloned.1.call-start = ((), (), s32[]{:S(2)}) async-start(), calls=%async_computation.4 | async-start | bytes 6684672 | tf_op jit(solution)/shard_map/all_gather | solution.py:38
  23.8 10.2 %copy-start.5 = (f32[1,128,8]{1,2,0:T(8,128)S(1)}, f32[1,128,8]{1,2,0:T(8,128)}, u32[]{:S(2)}) copy-start(f32[1,128,8]{1,2,0:T(8,128)} %param.11) | copy-start | bytes 12292
  27.8 64.3 %all-to-all-start = ((bf16[16,2,48,384]{3,2,1,0:T(8,128)(2,1)}), bf16[16,2,48,384]{3,2,1,0:T(8,128)(2,1)}, u32[]{:S(2)}, u32[]{:S(2)}) async-start(bf16[16,2,48,384]{3,2,1,0:T(8,128)(2,1)} %bitcast.2), calls=%async_computation | async-start | bytes 2359296 | tf_op jit(solution)/shard_map/all_to_all | solution.py:36
  34.0 217.2 %reduce-scatter.2.cloned.1.call-start = ((), (), s32[]{:S(2)}) async-start(), calls=%async_computation.2 | async-start | bytes 6684672 | tf_op jit(solution)/shard_map/reduce_scatter | solution.py:62
  114.2 11.9 %copy-start.2 = (bf16[1,2,1536,384]{2,3,1,0:T(8,128)(2,1)S(1)}, bf16[1,2,1536,384]{2,3,1,0:T(8,128)(2,1)}, u32[]{:S(2)}) copy-start(bf16[1,2,1536,384]{2,3,1,0:T(8,128)(2,1)} %copy.45) | copy-start | bytes 7077892
  124.5 1.6 copy-start.6
  133.1 36.2 %copy-start.3 = (bf16[1,2,1536,384]{2,3,1,0:T(8,128)(2,1)S(1)}, bf16[1,2,1536,384]{2,3,1,0:T(8,128)(2,1)}, u32[]{:S(2)}) copy-start(bf16[1,2,1536,384]{2,3,1,0:T(8,128)(2,1)} %copy.45) | copy-start | bytes 7077892
  251.1 13.3 %collective-permute-start.1 = (bf16[1,128,1536]{2,1,0:T(8,128)(2,1)}, bf16[1,128,1536]{2,1,0:T(8,128)(2,1)}, u32[]{:S(2)}, u32[]{:S(2)}) collective-permute-start(bf16[1,128,1536]{2,1,0:T(8,128)(2,1)} %bitcast.100), channel_id=1, source_target_pairs={{16,0},{0,16},{17,1},{1,17},{18,2},{2,18},{19,3},{3,19},{20,4},{4,... | collective-permute-start | bytes 1179656 | tf_op jit(solution)/shard_map/ppermute | solution.py:13
  258.5 7.7 %copy-start.1 = (bf16[1,2,384,1536]{3,2,1,0:T(8,128)(2,1)S(1)}, bf16[1,2,384,1536]{3,2,1,0:T(8,128)(2,1)}, u32[]{:S(2)}) copy-start(bf16[1,2,384,1536]{3,2,1,0:T(8,128)(2,1)} %param.13) | copy-start | bytes 7077892
Sparse Core Ops, SparseCore 0:
  20.5 80.3 all-gather.5
  103.2 60.1 all-gather.7
  167.3 83.7 reduce-scatter.1
where the time goes:
time: 274 us; the launch traced here: 273 us
  waiting for transfers between devices  91.5 us (33%)
  matrix products  69.7 us (25%)
  blocking collectives  45 us (16%)
  local copies, waits for them, and re-layouts  37.8 us (14%)
  between operations  13.9 us (5%)
  starting transfers between devices  10.8 us (4%)
  other arithmetic  4 us (1%)
    reduce_scatter x1, waiting for transfers between devices, body(): lax.psum_scatter(part.astype(BF16), 'ep', scatter_dimension=0, tiled=True)  51.1 us
    all_gather x1, blocking collectives, body(): routing_all = lax.all_gather(routing, 'ep', axis=0, tiled=False)  45 us
    dot_general x1, matrix products, body(): lax.dot_general(hidden, c_all, (((0,), (0,)), ((), ())), preferred_elemen...  30.7 us
    all_gather x1, waiting for transfers between devices, body(): x_all = lax.all_gather(inputs[0], 'ep', axis=0, tiled=True)  30.3 us
    unnamed x22, local copies, waits for them, and re-layouts  21.9 us
    dot_general x2, matrix products, body(): lax.dot_general(x_all, g[:, e * ff:(e + 1) * ff], (((0,), (0,)), ((), ())...  11.8 us
    reshape x1, local copies, waits for them, and re-layouts, body(): act = jax.nn.silu(gate).reshape(ep * toks, local, ff)  10.3 us
    dot_general x1, matrix products, body(): lax.dot_general(c_all, down_cat, (((1,), (1,)), ((), ())), preferred_elem...  10.2 us
  transfers between devices with their start and end apart: 6, of which 3 were waited for; matrix products, arithmetic and copies ran while one was open for 39% of the time, Pallas kernels for 0%

commit v1 on v0

--- a/solution.py
+++ b/solution.py
@@ -35,7 +35,12 @@
     gate_send = gate_send.astype(BF16).reshape(ep, local, cap, ff)
     gate_recv = lax.all_to_all(gate_send, "ep", split_axis=0, concat_axis=0, tiled=True)
     cot = from_behind(upstream, "section", -1)[0]
-    x_all = lax.all_gather(inputs[0], "ep", axis=0, tiled=True)
+    ring = [inputs[0]]
+    for hop in range(15):
+        ring.append(lax.ppermute(ring[-1], "ep", [(dev, (dev + 1) % 16) for dev in range(16)]))
+    x_all = jnp.roll(
+        jnp.concatenate(ring[::-1], axis=0), (lax.axis_index("ep") + 1) * ring[0].shape[0], axis=0
+    )
     c_all = lax.all_gather(cot, "ep", axis=0, tiled=True)
     me = lax.axis_index("ep")
     mine = (me * local + jnp.arange(local)).astype(F32)

time: 274 us -> 380 us (1.39)
  waiting for transfers between devices: 91.5 us -> 178 us
  local copies, waits for them, and re-layouts: 37.8 us -> 79 us
  blocking collectives: 45 us -> 20 us
    ppermute x0 -> x15, waiting for transfers between devices: none -> 147 us  [body(): lax.ppermute(ring[-1], 'ep', [(dev, (dev + 1) % 16) for dev in range(16)])]
    unnamed x22 -> x100, local copies, waits for them, and re-layouts: 21.9 us -> 60.9 us
    reduce_scatter x1, waiting for transfers between devices: 51.1 us -> 20.6 us  [body(): lax.psum_scatter(part.astype(BF16), 'ep', scatter_dimension=0, tiled=True)]
    all_gather x1 -> x0, waiting for transfers between devices: 30.3 us -> none  [body(): x_all = lax.all_gather(inputs[0], 'ep', axis=0, tiled=True)]
    all_gather x1, blocking collectives: 45 us -> 20 us  [body(): routing_all = lax.all_gather(routing, 'ep', axis=0, tiled=False)]
  transfers between devices with their start and end apart: 6 -> 20, of which waited for: 3 -> 14; matrix products, arithmetic and copies ran while one was open for 39% -> 34% of each run, Pallas kernels for 0% -> 0%
where the time goes in v1:
time: 380 us; the launch traced here: 378 us
  waiting for transfers between devices  178 us (47%)
  local copies, waits for them, and re-layouts  79 us (21%)
  matrix products  70.2 us (18%)
  blocking collectives  20 us (5%)
  between operations  14.3 us (4%)
  starting transfers between devices  11.2 us (3%)
  other arithmetic  5.74 us (2%)
    ppermute x15, waiting for transfers between devices, body(): lax.ppermute(ring[-1], 'ep', [(dev, (dev + 1) % 16) for dev in range(16)])  147 us
    unnamed x100, local copies, waits for them, and re-layouts  60.9 us
    dot_general x1, matrix products, body(): lax.dot_general(hidden, c_all, (((0,), (0,)), ((), ())), preferred_elemen...  29.3 us
    reduce_scatter x1, waiting for transfers between devices, body(): lax.psum_scatter(part.astype(BF16), 'ep', scatter_dimension=0, tiled=True)  20.6 us
    all_gather x1, blocking collectives, body(): routing_all = lax.all_gather(routing, 'ep', axis=0, tiled=False)  20 us
    dot_general x2, matrix products, body(): lax.dot_general(x_all, g[:, e * ff:(e + 1) * ff], (((0,), (0,)), ((), ())...  13.6 us
    reshape x1, local copies, waits for them, and re-layouts, body(): act = jax.nn.silu(gate).reshape(ep * toks, local, ff)  10.4 us
    dot_general x1, matrix products, body(): lax.dot_general(c_all, down_cat, (((1,), (1,)), ((), ())), preferred_elem...  10.2 us
  transfers between devices with their start and end apart: 20, of which 14 were waited for; matrix products, arithmetic and copies ran while one was open for 34% of the time, Pallas kernels for 0%

profile of v1, /device:TPU:0, one launch (start us, length us, event | category | flops | bytes accessed | tf_op | source)
XLA Modules:
  0.0 378.2 jit_solution(10983888891899841626)
XLA Ops:
  7.2 3.1 collective-permute-start
  10.3 9.3 %collective-permute-done = bf16[1,128,1536]{2,1,0:T(8,128)(2,1)S(1)} collective-permute-done((bf16[1,128,1536]{2,1,0:T(8,128)(2,1)}, bf16[1,128,1536]{2,1,0:T(8,128)(2,1)S(1)}, u32[]{:S(2)}, u32[]{:S(2)}) %collective-permute-start) | collective-permute-done | bytes 393248 | tf_op jit(solution)/shard_map/ppermute | solution.py:13
  20.5 10.1 %collective-permute-done.2 = bf16[128,1536]{1,0:T(8,128)(2,1)S(1)} collective-permute-done((bf16[128,1536]{1,0:T(8,128)(2,1)}, bf16[128,1536]{1,0:T(8,128)(2,1)S(1)}, u32[]{:S(2)}, u32[]{:S(2)}) %collective-permute-start.2) | collective-permute-done | bytes 393248 | tf_op jit(solution)/shard_map/ppermute | solution.py:40
  31.3 18.3 %collective-permute-done.3 = bf16[128,1536]{1,0:T(8,128)(2,1)S(1)} collective-permute-done((bf16[128,1536]{1,0:T(8,128)(2,1)S(1)}, bf16[128,1536]{1,0:T(8,128)(2,1)S(1)}, u32[]{:S(2)}, u32[]{:S(2)}) %collective-permute-start.3) | collective-permute-done | bytes 393248 | tf_op jit(solution)/shard_map/ppermute | solution.py:40
  50.3 10.1 %collective-permute-done.4 = bf16[128,1536]{1,0:T(8,128)(2,1)S(1)} collective-permute-done((bf16[128,1536]{1,0:T(8,128)(2,1)S(1)}, bf16[128,1536]{1,0:T(8,128)(2,1)S(1)}, u32[]{:S(2)}, u32[]{:S(2)}) %collective-permute-start.4) | collective-permute-done | bytes 393248 | tf_op jit(solution)/shard_map/ppermute | solution.py:40
  61.2 18.4 %collective-permute-done.5 = bf16[128,1536]{1,0:T(8,128)(2,1)S(1)} collective-permute-done((bf16[128,1536]{1,0:T(8,128)(2,1)S(1)}, bf16[128,1536]{1,0:T(8,128)(2,1)S(1)}, u32[]{:S(2)}, u32[]{:S(2)}) %collective-permute-start.5) | collective-permute-done | bytes 393248 | tf_op jit(solution)/shard_map/ppermute | solution.py:40
  80.4 17.0 %collective-permute-done.6 = bf16[128,1536]{1,0:T(8,128)(2,1)S(1)} collective-permute-done((bf16[128,1536]{1,0:T(8,128)(2,1)S(1)}, bf16[128,1536]{1,0:T(8,128)(2,1)S(1)}, u32[]{:S(2)}, u32[]{:S(2)}) %collective-permute-start.6) | collective-permute-done | bytes 393248 | tf_op jit(solution)/shard_map/ppermute | solution.py:40
  98.1 9.9 %collective-permute-done.7 = bf16[128,1536]{1,0:T(8,128)(2,1)S(1)} collective-permute-done((bf16[128,1536]{1,0:T(8,128)(2,1)S(1)}, bf16[128,1536]{1,0:T(8,128)(2,1)S(1)}, u32[]{:S(2)}, u32[]{:S(2)}) %collective-permute-start.7) | collective-permute-done | bytes 393248 | tf_op jit(solution)/shard_map/ppermute | solution.py:40
  109.5 9.2 %collective-permute-done.8 = bf16[128,1536]{1,0:T(8,128)(2,1)S(1)} collective-permute-done((bf16[128,1536]{1,0:T(8,128)(2,1)S(1)}, bf16[128,1536]{1,0:T(8,128)(2,1)S(1)}, u32[]{:S(2)}, u32[]{:S(2)}) %collective-permute-start.8) | collective-permute-done | bytes 393248 | tf_op jit(solution)/shard_map/ppermute | solution.py:40
  120.6 7.9 %collective-permute-done.9 = bf16[128,1536]{1,0:T(8,128)(2,1)S(1)} collective-permute-done((bf16[128,1536]{1,0:T(8,128)(2,1)S(1)}, bf16[128,1536]{1,0:T(8,128)(2,1)S(1)}, u32[]{:S(2)}, u32[]{:S(2)}) %collective-permute-start.9) | collective-permute-done | bytes 393248 | tf_op jit(solution)/shard_map/ppermute | solution.py:40
  128.6 4.1 %fusion.28 = bf16[1536,384]{1,0:T(8,128)(2,1)} fusion(s32[1024]{0:T(1024)S(1)} %add.36, bf16[1,128,8,384]{3,2,1,0:T(8,128)(2,1)} %param.9), kind=kOutput, calls=%fused_computation.24 | convolution fusion | flops 1210122240 | bytes 1970176 | tf_op jit(solution)/shard_map/dot_general | solution.py:34
  132.7 5.7 %all-to-all-start = ((bf16[16,2,48,384]{3,2,1,0:T(8,128)(2,1)}), bf16[16,2,48,384]{3,2,1,0:T(8,128)(2,1)}, u32[]{:S(2)}, u32[]{:S(2)}) async-start(bf16[16,2,48,384]{3,2,1,0:T(8,128)(2,1)} %bitcast.75), calls=%async_computation | async-start | bytes 2359296 | tf_op jit(solution)/shard_map/all_to_all | solution.py:36
  138.9 28.7 %collective-permute-done.11 = bf16[128,1536]{1,0:T(8,128)(2,1)S(1)} collective-permute-done((bf16[128,1536]{1,0:T(8,128)(2,1)S(1)}, bf16[128,1536]{1,0:T(8,128)(2,1)S(1)}, u32[]{:S(2)}, u32[]{:S(2)}) %collective-permute-start.11) | collective-permute-done | bytes 393248 | tf_op jit(solution)/shard_map/ppermute | solution.py:40
  168.4 10.0 %collective-permute-done.12 = bf16[128,1536]{1,0:T(8,128)(2,1)} collective-permute-done((bf16[128,1536]{1,0:T(8,128)(2,1)S(1)}, bf16[128,1536]{1,0:T(8,128)(2,1)}, u32[]{:S(2)}, u32[]{:S(2)}) %collective-permute-start.12) | collective-permute-done | bytes 393248 | tf_op jit(solution)/shard_map/ppermute | solution.py:40
  178.4 20.0 %all-gather = f32[2048,16]{0,1:T(8,128)S(1)} all-gather(f32[128,16]{0,1:T(8,128)S(1)} %pad_maximum_fusion.1), channel_id=2, replica_groups=mesh['section'=2,'ep'=16] {'ep'}, dimensions={0}, use_global_device_ids=true | all-gather | bytes 139264 | tf_op jit(solution)/shard_map/all_gather | solution.py:25
  200.1 1.0 compare_reduce_fusion
  201.0 7.6 %collective-permute-done.14 = bf16[128,1536]{1,0:T(8,128)(2,1)} collective-permute-done((bf16[128,1536]{1,0:T(8,128)(2,1)}, bf16[128,1536]{1,0:T(8,128)(2,1)}, u32[]{:S(2)}, u32[]{:S(2)}) %collective-permute-start.14) | collective-permute-done | bytes 393248 | tf_op jit(solution)/shard_map/ppermute | solution.py:40
  209.4 0.9 copy.46
  210.3 1.0 fusion.44
  211.7 4.8 %mul.48 = f32[2048,2,384]{2,1,0:T(2,128)S(1)} broadcast(f32[2048,2]{1,0:T(8,128)S(1)} %copy.40), dimensions={0,1} | broadcast | bytes 6307840 | tf_op jit(solution)/shard_map/mul | solution.py:56
  216.5 3.1 copy.49
  219.6 4.3 %copy.42 = bf16[1,2,1536,384]{2,3,1,0:T(8,128)(2,1)} copy(bf16[1,2,1536,384]{3,2,1,0:T(8,128)(2,1)} %param.12) | data formatting | bytes 4718592 | tf_op args[5]
  223.9 5.8 %bitcast_multiply_fusion = f32[16,128,2,384]{1,3,2,0:T(8,128)} fusion(bf16[16,2,48,384]{3,2,1,0:T(8,128)(2,1)} %all-to-all-done, f32[16,128,2]{1,2,0:T(2,128)S(1)} %copy-done.27, f32[48]{0:T(128)S(1)} %iota_convert_fusion), kind=kOutput, calls=%fused_computation.5 | convolution fusion | flops 157483008 | bytes 7487680 | tf_op jit(solution)/shard_map/stec,secf->stef/dot_general | solution.py:53
  229.7 10.4 %copy.43 = f32[16,128,2,384]{3,2,1,0:T(2,128)} copy(f32[16,128,2,384]{1,3,2,0:T(8,128)} %bitcast_multiply_fusion) | data formatting | bytes 12582912 | tf_op jit(solution)/shard_map/reshape | solution.py:54
  240.1 5.9 %copy.48 = f32[256,8,2,384]{3,1,2,0:T(8,128)} copy(f32[256,8,2,384]{3,2,1,0:T(2,128)} %bitcast.67) | data formatting | bytes 12582912
  246.0 0.8 constant_dynamic-update-slice_fusion.31
  246.9 1.8 constant_dynamic-update-slice_fusion.30
  248.6 1.8 constant_dynamic-update-slice_fusion.29
  250.4 1.8 constant_dynamic-update-slice_fusion.28
  252.2 1.8 constant_dynamic-update-slice_fusion.27
  254.0 0.8 constant_dynamic-update-slice_fusion.26
  254.8 10.2 %multiply_convert_fusion.1 = bf16[2048,768]{1,0:T(8,128)(2,1)S(1)} fusion(bf16[768,1536]{1,0:T(8,128)(2,1)S(1)} %bitcast.65, bf16[1,2048,1536]{2,1,0:T(8,128)(2,1)} %all-gather.4.cloned.1.call-done, f32[2048,768]{1,0:T(8,128)} %bitcast.70, f32[2048,768]{1,0:T(8,128)} %bitcast.68), kind=kOutput, calls=%fused_computation.11 | convolution fusion | flops 4836556800 | bytes 24379392 | tf_op jit(solution)/shard_map/dot_general | solution.py:64
  265.0 1.6 copy-done.29
  266.6 6.9 %convolution_convert_fusion = bf16[2048,1536]{1,0:T(8,128)(2,1)} fusion(bf16[2048,768]{1,0:T(8,128)(2,1)S(1)} %multiply_convert_fusion.1, bf16[1536,768]{0,1:T(8,128)(2,1)S(1)} %bitcast.72), kind=kOutput, calls=%fused_computation | convolution fusion | flops 4834983936 | bytes 11796480 | tf_op jit(solution)/shard_map/dot_general | solution.py:66
  273.6 1.9 constant_dynamic-update-slice_fusion.25
  275.5 0.8 constant_dynamic-update-slice_fusion.24
  276.3 0.8 constant_dynamic-update-slice_fusion.23
  277.1 0.8 constant_dynamic-update-slice_fusion.22
  277.9 0.8 constant_dynamic-update-slice_fusion.21
  278.6 0.8 constant_dynamic-update-slice_fusion.20
  279.4 0.8 constant_dynamic-update-slice_fusion.19
  280.2 0.8 constant_dynamic-update-slice_fusion.18
  281.0 0.8 constant_dynamic-update-slice_fusion.17
  281.8 0.8 constant_dynamic-update-slice_fusion.16
  282.6 1.8 constant_dynamic-update-slice_fusion.15
  284.4 1.8 constant_dynamic-update-slice_fusion.14
  286.2 1.8 constant_dynamic-update-slice_fusion.13
  288.0 1.8 constant_dynamic-update-slice_fusion.12
  289.9 1.8 constant_dynamic-update-slice_fusion.11
  291.7 1.8 constant_dynamic-update-slice_fusion.10
  293.5 0.8 constant_dynamic-update-slice_fusion.9
  294.3 0.8 constant_dynamic-update-slice_fusion.8
  295.8 0.8 constant_dynamic-update-slice_fusion.6
  296.6 0.8 constant_dynamic-update-slice_fusion.5
  297.4 1.9 constant_dynamic-update-slice_fusion.4
  299.3 1.8 constant_dynamic-update-slice_fusion.3
  301.8 0.8 constant_dynamic-update-slice_fusion.1
  302.6 0.8 constant_dynamic-update-slice_fusion
  303.4 6.9 %fusion.32 = bf16[1,1,1536,384]{3,2,1,0:T(8,128)(2,1)S(1)} fusion(bf16[4096,1536]{1,0:T(8,128)(2,1)} %constant_dynamic-update-slice_fusion, s32[]{:T(128)S(6)} %select_n.29, bf16[2048,768]{1,0:T(8,128)(2,1)S(1)} %copy-done.30), kind=kOutput, calls=%fused_computation.26 | convolution fusion | flops 2416508928 | bytes 9043972 | tf_op jit(solution)/shard_map/dot_general | solution.py:72
  310.4 29.3 %fusion.16 = bf16[768,1536]{1,0:T(8,128)(2,1)} fusion(bf16[1,2048,1536]{2,1,0:T(8,128)(2,1)} %all-gather.4.cloned.1.call-done, bf16[1536,768]{0,1:T(8,128)(2,1)S(1)} %bitcast.73, bf16[4096,1536]{1,0:T(8,128)(2,1)} %constant_dynamic-update-slice_fusion, s32[]{:T(128)S(6)} %select_n.29, f32[2048,768]{1,0:T(8,128)} %bitcast.71, f32[2048,768]{1,0:T(8,128)} %bitcast.69), kind=kOutput, calls=%fused_computation.20 | convolution fusion | flops 9669574656 | bytes 29884420 | tf_op jit(solution)/shard_map/dot_general | solution.py:69
  339.7 20.6 %reduce-scatter.2.cloned.1.call-done = bf16[128,1536]{1,0:T(8,128)(2,1)} async-done(((bf16[2048,1536]{1,0:T(8,128)(2,1)}), bf16[128,1536]{1,0:T(8,128)(2,1)}) %reduce-scatter.2.cloned.1.call-update) | async-done | bytes 393232 | tf_op jit(solution)/shard_map/reduce_scatter | solution.py:67
  360.3 1.4 collective-permute-start.1
  361.7 6.7 %fusion.29 = bf16[1,1,1536,384]{3,2,1,0:T(8,128)(2,1)S(1)} fusion(bf16[4096,1536]{1,0:T(8,128)(2,1)} %constant_dynamic-update-slice_fusion, s32[]{:T(128)S(6)} %select_n.29, bf16[2048,768]{1,0:T(8,128)(2,1)} %copy-done.29), kind=kOutput, calls=%fused_computation.25 | convolution fusion | flops 2416508928 | bytes 9043972 | tf_op jit(solution)/shard_map/dot_general | solution.py:72
  368.4 1.7 pad_maximum_fusion
  (109 shorter events, 15.0 us)
Async XLA Ops:
  7.2 247.6 %copy-start = (bf16[1,2,384,1536]{3,2,1,0:T(8,128)(2,1)S(1)}, bf16[1,2,384,1536]{3,2,1,0:T(8,128)(2,1)}, u32[]{:S(2)}) copy-start(bf16[1,2,384,1536]{3,2,1,0:T(8,128)(2,1)} %param.13) | copy-start | bytes 7077892
  7.2 171.2 %copy-start.28 = (f32[1,128,8]{1,2,0:T(8,128)S(1)}, f32[1,128,8]{1,2,0:T(8,128)}, u32[]{:S(2)}) copy-start(f32[1,128,8]{1,2,0:T(8,128)} %param.11) | copy-start | bytes 12292
  7.2 247.6 %all-gather.4.cloned.1.call-start = ((), (), s32[]{:S(2)}) async-start(), calls=%async_computation.3 | async-start | bytes 6684672 | tf_op jit(solution)/shard_map/all_gather | solution.py:44
  7.2 12.4 %collective-permute-start = (bf16[1,128,1536]{2,1,0:T(8,128)(2,1)}, bf16[1,128,1536]{2,1,0:T(8,128)(2,1)S(1)}, u32[]{:S(2)}, u32[]{:S(2)}) collective-permute-start(bf16[1,128,1536]{2,1,0:T(8,128)(2,1)} %param.8), channel_id=1, source_target_pairs={{16,0},{0,16},{17,1},{1,17},{18,2},{2,18},{19,3},{3,19},{20,4},{4,... | collective-permute-start | bytes 1179656 | tf_op jit(solution)/shard_map/ppermute | solution.py:13
  19.6 0.7 copy-start.26
  20.4 10.2 %collective-permute-start.2 = (bf16[128,1536]{1,0:T(8,128)(2,1)}, bf16[128,1536]{1,0:T(8,128)(2,1)S(1)}, u32[]{:S(2)}, u32[]{:S(2)}) collective-permute-start(bf16[128,1536]{1,0:T(8,128)(2,1)} %bitcast.74), channel_id=1, source_target_pairs={{0,1},{1,2},{2,3},{3,4},{4,5},{5,6},{6,7},{7,8},{8,9},{9,10},{10,1... | collective-permute-start | bytes 1179656 | tf_op jit(solution)/shard_map/ppermute | solution.py:40
  30.6 0.7 copy-start.5
  31.3 18.3 %collective-permute-start.3 = (bf16[128,1536]{1,0:T(8,128)(2,1)S(1)}, bf16[128,1536]{1,0:T(8,128)(2,1)S(1)}, u32[]{:S(2)}, u32[]{:S(2)}) collective-permute-start(bf16[128,1536]{1,0:T(8,128)(2,1)S(1)} %collective-permute-done.2), channel_id=1, source_target_pairs={{0,1},{1,2},{2,3},{3,4},{4,5},{5,6},{6,7},{7,8},{8,9},{9,10},{10,1... | collective-permute-start | bytes 1179656 | tf_op jit(solution)/shard_map/ppermute | solution.py:40
  49.6 0.8 copy-start.7
  50.3 10.1 %collective-permute-start.4 = (bf16[128,1536]{1,0:T(8,128)(2,1)S(1)}, bf16[128,1536]{1,0:T(8,128)(2,1)S(1)}, u32[]{:S(2)}, u32[]{:S(2)}) collective-permute-start(bf16[128,1536]{1,0:T(8,128)(2,1)S(1)} %collective-permute-done.3), channel_id=1, source_target_pairs={{0,1},{1,2},{2,3},{3,4},{4,5},{5,6},{6,7},{7,8},{8,9},{9,10},{10,1... | collective-permute-start | bytes 1179656 | tf_op jit(solution)/shard_map/ppermute | solution.py:40
  60.4 0.8 copy-start.9
  61.2 18.4 %collective-permute-start.5 = (bf16[128,1536]{1,0:T(8,128)(2,1)S(1)}, bf16[128,1536]{1,0:T(8,128)(2,1)S(1)}, u32[]{:S(2)}, u32[]{:S(2)}) collective-permute-start(bf16[128,1536]{1,0:T(8,128)(2,1)S(1)} %collective-permute-done.4), channel_id=1, source_target_pairs={{0,1},{1,2},{2,3},{3,4},{4,5},{5,6},{6,7},{7,8},{8,9},{9,10},{10,1... | collective-permute-start | bytes 1179656 | tf_op jit(solution)/shard_map/ppermute | solution.py:40
  79.6 0.8 copy-start.11
  80.4 17.0 %collective-permute-start.6 = (bf16[128,1536]{1,0:T(8,128)(2,1)S(1)}, bf16[128,1536]{1,0:T(8,128)(2,1)S(1)}, u32[]{:S(2)}, u32[]{:S(2)}) collective-permute-start(bf16[128,1536]{1,0:T(8,128)(2,1)S(1)} %collective-permute-done.5), channel_id=1, source_target_pairs={{0,1},{1,2},{2,3},{3,4},{4,5},{5,6},{6,7},{7,8},{8,9},{9,10},{10,1... | collective-permute-start | bytes 1179656 | tf_op jit(solution)/shard_map/ppermute | solution.py:40
  97.4 0.7 copy-start.13
  98.1 9.9 %collective-permute-start.7 = (bf16[128,1536]{1,0:T(8,128)(2,1)S(1)}, bf16[128,1536]{1,0:T(8,128)(2,1)S(1)}, u32[]{:S(2)}, u32[]{:S(2)}) collective-permute-start(bf16[128,1536]{1,0:T(8,128)(2,1)S(1)} %collective-permute-done.6), channel_id=1, source_target_pairs={{0,1},{1,2},{2,3},{3,4},{4,5},{5,6},{6,7},{7,8},{8,9},{9,10},{10,1... | collective-permute-start | bytes 1179656 | tf_op jit(solution)/shard_map/ppermute | solution.py:40
  108.0 0.8 copy-start.15
  108.8 9.9 %collective-permute-start.8 = (bf16[128,1536]{1,0:T(8,128)(2,1)S(1)}, bf16[128,1536]{1,0:T(8,128)(2,1)S(1)}, u32[]{:S(2)}, u32[]{:S(2)}) collective-permute-start(bf16[128,1536]{1,0:T(8,128)(2,1)S(1)} %collective-permute-done.7), channel_id=1, source_target_pairs={{0,1},{1,2},{2,3},{3,4},{4,5},{5,6},{6,7},{7,8},{8,9},{9,10},{10,1... | collective-permute-start | bytes 1179656 | tf_op jit(solution)/shard_map/ppermute | solution.py:40
  118.7 92.6 %copy-start.17 = (bf16[128,1536]{1,0:T(8,128)(2,1)}, bf16[128,1536]{1,0:T(8,128)(2,1)S(1)}, u32[]{:S(2)}) copy-start(bf16[128,1536]{1,0:T(8,128)(2,1)S(1)} %collective-permute-done.8) | copy-start | bytes 1179652
  118.7 9.9 %collective-permute-start.9 = (bf16[128,1536]{1,0:T(8,128)(2,1)S(1)}, bf16[128,1536]{1,0:T(8,128)(2,1)S(1)}, u32[]{:S(2)}, u32[]{:S(2)}) collective-permute-start(bf16[128,1536]{1,0:T(8,128)(2,1)S(1)} %collective-permute-done.8), channel_id=1, source_target_pairs={{0,1},{1,2},{2,3},{3,4},{4,5},{5,6},{6,7},{7,8},{8,9},{9,10},{10,1... | collective-permute-start | bytes 1179656 | tf_op jit(solution)/shard_map/ppermute | solution.py:40
  128.6 82.7 %copy-start.19 = (bf16[128,1536]{1,0:T(8,128)(2,1)}, bf16[128,1536]{1,0:T(8,128)(2,1)S(1)}, u32[]{:S(2)}) copy-start(bf16[128,1536]{1,0:T(8,128)(2,1)S(1)} %collective-permute-done.9) | copy-start | bytes 1179652
  128.6 9.9 %collective-permute-start.10 = (bf16[128,1536]{1,0:T(8,128)(2,1)S(1)}, bf16[128,1536]{1,0:T(8,128)(2,1)S(1)}, u32[]{:S(2)}, u32[]{:S(2)}) collective-permute-start(bf16[128,1536]{1,0:T(8,128)(2,1)S(1)} %collective-permute-done.9), channel_id=1, source_target_pairs={{0,1},{1,2},{2,3},{3,4},{4,5},{5,6},{6,7},{7,8},{8,9},{9,10},{10,1... | collective-permute-start | bytes 1179656 | tf_op jit(solution)/shard_map/ppermute | solution.py:40
  132.7 91.2 %all-to-all-start = ((bf16[16,2,48,384]{3,2,1,0:T(8,128)(2,1)}), bf16[16,2,48,384]{3,2,1,0:T(8,128)(2,1)}, u32[]{:S(2)}, u32[]{:S(2)}) async-start(bf16[16,2,48,384]{3,2,1,0:T(8,128)(2,1)} %bitcast.75), calls=%async_computation | async-start | bytes 2359296 | tf_op jit(solution)/shard_map/all_to_all | solution.py:36
  138.4 221.9 %reduce-scatter.2.cloned.1.call-start = ((), (), s32[]{:S(2)}) async-start(), calls=%async_computation.2 | async-start | bytes 6684672 | tf_op jit(solution)/shard_map/reduce_scatter | solution.py:67
  138.5 72.8 %copy-start.21 = (bf16[128,1536]{1,0:T(8,128)(2,1)}, bf16[128,1536]{1,0:T(8,128)(2,1)S(1)}, u32[]{:S(2)}) copy-start(bf16[128,1536]{1,0:T(8,128)(2,1)S(1)} %collective-permute-done.10) | copy-start | bytes 1179652
  138.5 29.1 %collective-permute-start.11 = (bf16[128,1536]{1,0:T(8,128)(2,1)S(1)}, bf16[128,1536]{1,0:T(8,128)(2,1)S(1)}, u32[]{:S(2)}, u32[]{:S(2)}) collective-permute-start(bf16[128,1536]{1,0:T(8,128)(2,1)S(1)} %collective-permute-done.10), channel_id=1, source_target_pairs={{0,1},{1,2},{2,3},{3,4},{4,5},{5,6},{6,7},{7,8},{8,9},{9,10},{10,1... | collective-permute-start | bytes 1179656 | tf_op jit(solution)/shard_map/ppermute | solution.py:40
  167.6 0.8 copy-start.23
  168.4 10.0 %collective-permute-start.12 = (bf16[128,1536]{1,0:T(8,128)(2,1)S(1)}, bf16[128,1536]{1,0:T(8,128)(2,1)}, u32[]{:S(2)}, u32[]{:S(2)}) collective-permute-start(bf16[128,1536]{1,0:T(8,128)(2,1)S(1)} %collective-permute-done.11), channel_id=1, source_target_pairs={{0,1},{1,2},{2,3},{3,4},{4,5},{5,6},{6,7},{7,8},{8,9},{9,10},{10,1... | collective-permute-start | bytes 1179656 | tf_op jit(solution)/shard_map/ppermute | solution.py:40
  178.4 20.0 %collective-permute-start.13 = (bf16[128,1536]{1,0:T(8,128)(2,1)}, bf16[128,1536]{1,0:T(8,128)(2,1)}, u32[]{:S(2)}, u32[]{:S(2)}) collective-permute-start(bf16[128,1536]{1,0:T(8,128)(2,1)} %collective-permute-done.12), channel_id=1, source_target_pairs={{0,1},{1,2},{2,3},{3,4},{4,5},{5,6},{6,7},{7,8},{8,9},{9,10},{10,1... | collective-permute-start | bytes 1179656 | tf_op jit(solution)/shard_map/ppermute | solution.py:40
  198.4 10.3 %collective-permute-start.14 = (bf16[128,1536]{1,0:T(8,128)(2,1)}, bf16[128,1536]{1,0:T(8,128)(2,1)}, u32[]{:S(2)}, u32[]{:S(2)}) collective-permute-start(bf16[128,1536]{1,0:T(8,128)(2,1)} %collective-permute-done.13), channel_id=1, source_target_pairs={{0,1},{1,2},{2,3},{3,4},{4,5},{5,6},{6,7},{7,8},{8,9},{9,10},{10,1... | collective-permute-start | bytes 1179656 | tf_op jit(solution)/shard_map/ppermute | solution.py:40
  208.7 15.2 %collective-permute-start.15 = (bf16[128,1536]{1,0:T(8,128)(2,1)}, bf16[128,1536]{1,0:T(8,128)(2,1)}, u32[]{:S(2)}, u32[]{:S(2)}) collective-permute-start(bf16[128,1536]{1,0:T(8,128)(2,1)} %collective-permute-done.14), channel_id=1, source_target_pairs={{0,1},{1,2},{2,3},{3,4},{4,5},{5,6},{6,7},{7,8},{8,9},{9,10},{10,1... | collective-permute-start | bytes 1179656 | tf_op jit(solution)/shard_map/ppermute | solution.py:40
  211.7 12.2 %copy-start.27 = (f32[16,128,2]{1,2,0:T(2,128)S(1)}, f32[16,128,2]{1,2,0:T(2,128)}, u32[]{:S(2)}) copy-start(f32[16,128,2]{1,2,0:T(2,128)} %copy.37) | copy-start | bytes 49156
  223.9 22.2 %collective-permute-start.16 = (bf16[128,1536]{1,0:T(8,128)(2,1)}, bf16[128,1536]{1,0:T(8,128)(2,1)S(1)}, u32[]{:S(2)}, u32[]{:S(2)}) collective-permute-start(bf16[128,1536]{1,0:T(8,128)(2,1)} %collective-permute-done.15), channel_id=1, source_target_pairs={{0,1},{1,2},{2,3},{3,4},{4,5},{5,6},{6,7},{7,8},{8,9},{9,10},{10,1... | collective-permute-start | bytes 1179656 | tf_op jit(solution)/shard_map/ppermute | solution.py:40
  229.7 24.3 %copy-start.24 = (bf16[128,1536]{1,0:T(8,128)(2,1)S(1)}, bf16[128,1536]{1,0:T(8,128)(2,1)}, u32[]{:S(2)}) copy-start(bf16[128,1536]{1,0:T(8,128)(2,1)} %copy-done.23) | copy-start | bytes 1179652
  246.0 18.9 %copy-start.25 = (bf16[128,1536]{1,0:T(8,128)(2,1)}, bf16[128,1536]{1,0:T(8,128)(2,1)S(1)}, u32[]{:S(2)}) copy-start(bf16[128,1536]{1,0:T(8,128)(2,1)S(1)} %collective-permute-done.16) | copy-start | bytes 1179652
  254.7 11.8 %copy-start.2 = (bf16[1,2,1536,384]{2,3,1,0:T(8,128)(2,1)S(1)}, bf16[1,2,1536,384]{2,3,1,0:T(8,128)(2,1)}, u32[]{:S(2)}) copy-start(bf16[1,2,1536,384]{2,3,1,0:T(8,128)(2,1)} %copy.42) | copy-start | bytes 7077892
  264.9 1.6 copy-start.29
  266.6 9.0 %copy-start.20 = (bf16[128,1536]{1,0:T(8,128)(2,1)S(1)}, bf16[128,1536]{1,0:T(8,128)(2,1)}, u32[]{:S(2)}) copy-start(bf16[128,1536]{1,0:T(8,128)(2,1)} %copy-done.19) | copy-start | bytes 1179652
  266.6 9.8 %copy-start.18 = (bf16[128,1536]{1,0:T(8,128)(2,1)S(1)}, bf16[128,1536]{1,0:T(8,128)(2,1)}, u32[]{:S(2)}) copy-start(bf16[128,1536]{1,0:T(8,128)(2,1)} %copy-done.17) | copy-start | bytes 1179652
  266.6 10.5 %copy-start.16 = (bf16[128,1536]{1,0:T(8,128)(2,1)S(1)}, bf16[128,1536]{1,0:T(8,128)(2,1)}, u32[]{:S(2)}) copy-start(bf16[128,1536]{1,0:T(8,128)(2,1)} %copy-done.15) | copy-start | bytes 1179652
  266.6 11.3 %copy-start.14 = (bf16[128,1536]{1,0:T(8,128)(2,1)S(1)}, bf16[128,1536]{1,0:T(8,128)(2,1)}, u32[]{:S(2)}) copy-start(bf16[128,1536]{1,0:T(8,128)(2,1)} %copy-done.13) | copy-start | bytes 1179652
  266.6 12.1 %copy-start.12 = (bf16[128,1536]{1,0:T(8,128)(2,1)S(1)}, bf16[128,1536]{1,0:T(8,128)(2,1)}, u32[]{:S(2)}) copy-start(bf16[128,1536]{1,0:T(8,128)(2,1)} %copy-done.11) | copy-start | bytes 1179652
  266.6 12.8 %copy-start.10 = (bf16[128,1536]{1,0:T(8,128)(2,1)S(1)}, bf16[128,1536]{1,0:T(8,128)(2,1)}, u32[]{:S(2)}) copy-start(bf16[128,1536]{1,0:T(8,128)(2,1)} %copy-done.9) | copy-start | bytes 1179652
  266.6 13.6 %copy-start.8 = (bf16[128,1536]{1,0:T(8,128)(2,1)S(1)}, bf16[128,1536]{1,0:T(8,128)(2,1)}, u32[]{:S(2)}) copy-start(bf16[128,1536]{1,0:T(8,128)(2,1)} %copy-done.7) | copy-start | bytes 1179652
  273.5 7.5 %copy-start.6 = (bf16[128,1536]{1,0:T(8,128)(2,1)S(1)}, bf16[128,1536]{1,0:T(8,128)(2,1)}, u32[]{:S(2)}) copy-start(bf16[128,1536]{1,0:T(8,128)(2,1)} %copy-done.5) | copy-start | bytes 1179652
  273.5 8.3 %copy-start.4 = (bf16[1,128,1536]{2,1,0:T(8,128)(2,1)S(1)}, bf16[1,128,1536]{2,1,0:T(8,128)(2,1)}, u32[]{:S(2)}) copy-start(bf16[1,128,1536]{2,1,0:T(8,128)(2,1)} %param.7) | copy-start | bytes 1179652
  273.6 20.0 %copy-start.22 = (bf16[128,1536]{1,0:T(8,128)(2,1)S(1)}, bf16[128,1536]{1,0:T(8,128)(2,1)}, u32[]{:S(2)}) copy-start(bf16[128,1536]{1,0:T(8,128)(2,1)} %copy-done.21) | copy-start | bytes 1179652
  273.6 29.9 %copy-start.30 = (bf16[2048,768]{1,0:T(8,128)(2,1)S(1)}, bf16[2048,768]{1,0:T(8,128)(2,1)}, u32[]{:S(2)}) copy-start(bf16[2048,768]{1,0:T(8,128)(2,1)} %copy-done.29) | copy-start | bytes 9437188
  297.4 13.0 %copy-start.3 = (bf16[1,2,1536,384]{2,3,1,0:T(8,128)(2,1)S(1)}, bf16[1,2,1536,384]{2,3,1,0:T(8,128)(2,1)}, u32[]{:S(2)}) copy-start(bf16[1,2,1536,384]{2,3,1,0:T(8,128)(2,1)} %copy.42) | copy-start | bytes 7077892
  360.3 11.1 %copy-start.1 = (bf16[1,2,384,1536]{3,2,1,0:T(8,128)(2,1)S(1)}, bf16[1,2,384,1536]{3,2,1,0:T(8,128)(2,1)}, u32[]{:S(2)}) copy-start(bf16[1,2,384,1536]{3,2,1,0:T(8,128)(2,1)} %param.13) | copy-start | bytes 7077892
  360.3 10.3 %collective-permute-start.1 = (bf16[1,128,1536]{2,1,0:T(8,128)(2,1)}, bf16[1,128,1536]{2,1,0:T(8,128)(2,1)S(1)}, u32[]{:S(2)}, u32[]{:S(2)}) collective-permute-start(bf16[1,128,1536]{2,1,0:T(8,128)(2,1)} %bitcast.82), channel_id=1, source_target_pairs={{16,0},{0,16},{17,1},{1,17},{18,2},{2,18},{19,3},{3,19},{20,4},{4,... | collective-permute-start | bytes 1179656 | tf_op jit(solution)/shard_map/ppermute | solution.py:13
Sparse Core Ops, SparseCore 0:
  20.5 71.2 all-gather.3
  273.7 86.5 reduce-scatter.1
